TPU v7x, 768 devices: a whole 4x8x12 slice. The times are simulated.
768 devices in a mesh: dp: 12 (over x, z_lo), expert: 64 (over y, z_hi, core).
Axes of the slice: x: 4, y: 8, z: 12 (z_hi: 4, z_lo: 3; z = z_hi * 3 + z_lo), core: 2. Of those that a mesh axis runs over, the one named last changes fastest.
Arguments:
- out_grad: bfloat16 [9216, 3072], P(('dp', 'expert')), may hold values from -6 to 6
- layer_input: bfloat16 [9216, 3072], P(('dp', 'expert')), may hold values from -6 to 6
- expert_ids: int32 [9216, 2], P(('dp', 'expert')), may hold values from 0 to 7, as said below
- gate_prob: float32 [9216, 2], P(('dp', 'expert')), may hold values from 0.05 to 1
- w_stack: bfloat16 [3, 3072, 8192], P(None, 'dp', 'expert'), may hold values from -0.109375 to 0.109375
- scale_exps: int32 [3, 24, 64], P(None, 'dp', 'expert'), may hold values from -1 to 1
Outputs:
- input_grad: bfloat16 [9216, 3072], P(('dp', 'expert'))
- weight_grads: float32 [3, 3072, 8192], P(None, 'dp', 'expert')
Inputs may be any that keep to these rules, and one draw needn't show every extreme that they name: `expert_ids`: each row names two different experts. In each aligned block of 12 rows (the tokens of one device) between 1 and 3 rows name expert 0, and some blocks have exactly 3 in every draw.
All inputs are finite; a program needn't handle non-finite values.
Results may differ from a plain program's by a relative error of at most 0.015.
Values may be sent and summed in bfloat16 or wider, within the bound.
A program may use at most 32 MiB of HBM per device.

v0:
```python
import jax
import jax.numpy as jnp
from jax import lax
from jax.sharding import Mesh
from jax.sharding import PartitionSpec as P

TILE = 128
CAP = 3
EXPERT = ("expert_0", "expert_1", "expert_2")
DP_EXPERT = ("dp", "expert_0", "expert_1", "expert_2")


def sent_together(arrays, axis, dim, along):
    widths = [a.shape[along] for a in arrays]
    both = jnp.concatenate(arrays, axis=along)
    filled = lax.all_gather(both, axis, axis=dim, tiled=True)
    return tuple(jnp.split(filled, [sum(widths[:k]) for k in range(1, len(widths))], axis=along))


def copy_for_each(x, axis):
    length = lax.axis_size(axis)
    return lax.all_to_all(jnp.broadcast_to(x[None], (length, *x.shape)), axis, 0, 0, tiled=True)


def joined_along(pieces, dim):
    dims = list(pieces.shape[1:])
    dims[dim] *= pieces.shape[0]
    return jnp.moveaxis(pieces, 0, dim).reshape(dims)


def gather_directly(x, axis, dim):
    pieces = copy_for_each(x, axis)
    return joined_along(pieces, dim)


def split_up(x, dim, length):
    before, after = (x.shape[:dim], x.shape[dim + 1 :])
    return jnp.moveaxis(x.reshape(*before, length, -1, *after), dim, 0)


def scatter_pairs(x, chips, core, dim):
    sizes = (lax.axis_size(chips), lax.axis_size(core))
    pieces = split_up(x, dim, sizes[0] * sizes[1])
    inside = pieces.shape[1:]
    pieces = pieces.reshape(*sizes, *inside).swapaxes(0, 1).reshape(-1, *inside)
    pieces = lax.psum_scatter(pieces, core, scatter_dimension=0, tiled=True)
    return lax.psum_scatter(pieces, chips, scatter_dimension=0, tiled=True)[0]


def sum_at_owner(x, axis, dim):
    pieces = split_up(x, dim, lax.axis_size(axis))
    arrived = lax.all_to_all(pieces, axis, split_axis=0, concat_axis=0, tiled=True)
    return arrived.astype(jnp.float32).sum(axis=0)


def contract_rows(left, right):
    return lax.dot_general(
        left, right, (((0,), (0,)), ((), ())), preferred_element_type=jnp.float32
    )


def back_project(grad_rows, matrix):
    return lax.dot_general(
        grad_rows, matrix, (((1,), (1,)), ((), ())), preferred_element_type=jnp.float32
    )


def per_device(out_grad, layer_input, expert_ids, gate_prob, w_stack, scale_exps):
    tok_count = out_grad.shape[0]
    routed = expert_ids == 0
    routed_mask = jnp.any(routed, axis=1)
    expert_prob = jnp.sum(jnp.where(routed, gate_prob, 0.0), axis=1)
    slot_index = jnp.cumsum(routed_mask.astype(jnp.int32)) - 1
    places = jnp.arange(CAP, dtype=jnp.int32)
    slot_hit = (slot_index[None, :] == places[:, None]) & routed_mask[None, :]
    source = jnp.sum(
        jnp.where(slot_hit, jnp.arange(tok_count, dtype=jnp.int32)[None, :], 0), axis=1
    )
    slot_valid = jnp.any(slot_hit, axis=1)
    sent_input = jnp.where(slot_valid[:, None], layer_input[source], jnp.zeros((), jnp.bfloat16))
    sent_grad = jnp.where(
        slot_valid[:, None],
        expert_prob[source][:, None] * out_grad[source].astype(jnp.float32),
        0.0,
    ).astype(jnp.bfloat16)
    routed_input, routed_grad = sent_together((sent_input, sent_grad), EXPERT, 0, 1)
    local_shape = w_stack.shape
    factor = jnp.exp2(scale_exps.astype(jnp.float32))
    scaled = (
        w_stack.astype(jnp.float32).reshape(
            3, local_shape[1] // TILE, TILE, local_shape[2] // TILE, TILE
        )
        * factor[:, :, None, :, None]
    )
    weights = gather_directly(scaled.reshape(local_shape).astype(jnp.bfloat16), "dp", 1)
    gate_value = jnp.dot(routed_input, weights[0], preferred_element_type=jnp.float32)
    up_value = jnp.dot(routed_input, weights[1], preferred_element_type=jnp.float32)
    down_back = jnp.dot(routed_grad, weights[2], preferred_element_type=jnp.float32)
    gate_sigmoid = jax.nn.sigmoid(gate_value)
    gate_act = gate_value * gate_sigmoid
    gate_grad = (
        down_back * up_value * gate_sigmoid * (1.0 + gate_value * (1.0 - gate_sigmoid))
    ).astype(jnp.bfloat16)
    up_grad = (down_back * gate_act).astype(jnp.bfloat16)
    hidden = (gate_act * up_value).astype(jnp.bfloat16)
    returned = scatter_pairs(
        back_project(gate_grad, weights[0]) + back_project(up_grad, weights[1]),
        ("expert_0", "expert_1"),
        "expert_2",
        0,
    )
    picked = returned[jnp.clip(slot_index, 0, CAP - 1)]
    input_grad = jnp.where(routed_mask[:, None], picked, 0.0).astype(jnp.bfloat16)
    partial_value = jnp.stack(
        [
            contract_rows(routed_input, gate_grad),
            contract_rows(routed_input, up_grad),
            contract_rows(routed_grad, hidden),
        ]
    )
    weight_grads = sum_at_owner(partial_value.astype(jnp.bfloat16), "dp", 1)
    return (input_grad, weight_grads)


def solution(mesh):
    split = Mesh(
        mesh.devices.reshape(mesh.shape["dp"], 8, 4, 2), ("dp", "expert_0", "expert_1", "expert_2")
    )
    in_specs = (
        P(DP_EXPERT, None),
        P(DP_EXPERT, None),
        P(DP_EXPERT, None),
        P(DP_EXPERT, None),
        P(None, "dp", EXPERT),
        P(None, "dp", EXPERT),
    )
    out_specs = (P(DP_EXPERT, None), P(None, "dp", EXPERT))
    return jax.shard_map(
        per_device, mesh=split, in_specs=in_specs, out_specs=out_specs, check_vma=False
    )
```

profile of v0, /device:TPU:128, one launch (start us, length us, event | category | flops | bytes accessed | tf_op | source)
XLA Modules:
  0.0 424.5 jit_solution(17581043269656391912)
XLA Ops:
  7.2 0.0 copy-start
  7.2 0.7 multiply_exponential_fusion
  7.9 0.1 copy.22
  8.0 0.1 broadcast_bitcast_fusion
  8.1 1.1 multiply_convert_fusion
  9.2 2.0 broadcast_in_dim.76
  11.2 0.0 copy-start.5
  11.2 0.0 copy-start.6
  11.2 0.0 copy-start.4
  11.2 11.4 %all-to-all-start = ((bf16[12,3,256,128]{3,2,1,0:T(8,128)(2,1)}), bf16[12,3,256,128]{3,2,1,0:T(8,128)(2,1)S(1)}, u32[]{:S(2)}, u32[]{:S(2)}) async-start(bf16[12,3,256,128]{3,2,1,0:T(8,128)(2,1)} %broadcast_in_dim.76), calls=%async_computation | async-start | bytes 4718592 | tf_op jit(solution)/shard_map/all_to_all | solution.py:22
  22.6 0.0 all-gather.3.cloned.1.call-start
  22.6 0.0 copy-done.5
  22.7 0.2 reduce-window.4
  22.9 0.1 select_reduce_fusion
  23.0 0.1 fusion.12
  23.1 0.0 copy-done.6
  23.1 0.0 copy-done
  23.1 0.6 gather_fusion.2
  23.7 0.6 gather_fusion.1
  24.4 0.0 copy-done.4
  24.4 0.6 gather_fusion
  24.9 0.1 broadcast_select_fusion
  25.0 0.1 select_convert_fusion.1
  25.1 0.6 maximum_bitcast_fusion.1
  25.8 0.0 all-gather.3.cloned.1.call-update
  25.8 100.0 %all-gather.3.cloned.1.call-done = bf16[64,3,6144]{2,1,0:T(4,128)(2,1)} async-done(((bf16[1,3,6144]{2,1,0:T(4,128)(2,1)}), bf16[64,3,6144]{2,1,0:T(4,128)(2,1)}) %all-gather.3.cloned.1.call-update) | async-done | bytes 2359312 | tf_op jit(solution)/shard_map/all_gather | solution.py:16
  125.7 6.8 %reshape.122 = bf16[192,6144]{1,0:T(8,128)(2,1)} reshape(bf16[64,3,6144]{2,1,0:T(4,128)(2,1)} %all-gather.3.cloned.1.call-done) | data formatting | bytes 4718592
  132.5 0.0 all-to-all-done
  132.5 0.0 copy-start.1
  132.5 0.2 fusion.17
  132.7 0.0 copy-start.2
  132.7 1.7 copy-done.1
  134.5 0.5 fusion.7
  134.9 0.5 fusion.5
  135.4 0.6 convolution_convert_fusion
  136.1 0.0 copy-done.2
  136.1 0.5 multiply_convert_fusion.2
  136.6 0.6 convolution_convert_fusion.2
  137.2 0.6 convolution_convert_fusion.1
  137.8 1.7 maximum_bitcast_fusion
  139.6 6.7 %all-to-all-start.1 = ((bf16[12,3,256,128]{3,2,1,0:T(8,128)(2,1)}), bf16[12,3,256,128]{3,2,1,0:T(8,128)(2,1)}, u32[]{:S(2)}, u32[]{:S(2)}) async-start(bf16[12,3,256,128]{3,2,1,0:T(8,128)(2,1)} %maximum_bitcast_fusion), calls=%async_computation.1 | async-start | bytes 4718592 | tf_op jit(solution)/shard_map/all_to_all | solution.py:52
  146.3 0.0 copy-start.3
  146.3 0.0 all-reduce.5.cloned.1.call-start
  146.3 0.5 fusion.18
  146.8 0.6 copy-done.3
  147.4 1.9 convolution_add_fusion
  149.3 3.0 reshape_reshape.3
  152.3 1.4 copy.23
  153.7 3.3 copy.24
  157.0 0.0 all-reduce.5.cloned.1.call-update
  157.0 1.3 dynamic-slice
  158.3 1.3 dynamic-slice.2
  160.2 39.2 %all-reduce.5.cloned.1.call-done = f32[64,3,3072]{2,1,0:T(4,128)} async-done(((f32[64,3,3072]{2,1,0:T(4,128)}), f32[64,3,3072]{2,1,0:T(4,128)}) %all-reduce.5.cloned.1.call-update) | async-done | bytes 2359312
  199.4 1.7 constant_dynamic-slice_fusion
  201.1 211.8 %all-reduce.6 = bf16[32,3,3072]{2,1,0:T(4,128)(2,1)S(1)} all-reduce(f32[32,3,3072]{2,1,0:T(4,128)S(1)} %constant_dynamic-slice_fusion), channel_id=3, replica_groups=mesh['dp'=12,'expert_0'=8,'expert_1'=4,'expert_2'=2] {'expert_0','expert..., use_global_device_ids=true, to_apply=%region_6.7.clone | all-reduce | flops 294912 | bytes 1769472
  412.9 0.7 dynamic-slice_bitcast_fusion
  413.6 0.6 gather_fusion.3
  414.2 0.7 select_convert_fusion
  414.9 0.0 all-to-all-done.1
  414.9 2.8 convert_reduce_fusion
  (8 shorter events, 0.1 us)
Async XLA Ops:
  7.2 16.0 %copy-start = (bf16[12,3072]{1,0:T(8,128)(2,1)S(1)}, bf16[12,3072]{1,0:T(8,128)(2,1)}, u32[]{:S(2)}) copy-start(bf16[12,3072]{1,0:T(8,128)(2,1)} %param.6) | copy-start | bytes 221188
  11.2 11.5 %copy-start.5 = (s32[12,2]{0,1:T(2,128)S(1)}, s32[12,2]{0,1:T(2,128)}, u32[]{:S(2)}) copy-start(s32[12,2]{0,1:T(2,128)} %param.8) | copy-start | bytes 292
  11.2 11.9 %copy-start.6 = (f32[12,2]{0,1:T(2,128)S(1)}, f32[12,2]{0,1:T(2,128)}, u32[]{:S(2)}) copy-start(f32[12,2]{0,1:T(2,128)} %param.9) | copy-start | bytes 292
  11.2 13.2 %copy-start.4 = (bf16[12,3072]{1,0:T(8,128)(2,1)S(1)}, bf16[12,3072]{1,0:T(8,128)(2,1)}, u32[]{:S(2)}) copy-start(bf16[12,3072]{1,0:T(8,128)(2,1)} %param.7) | copy-start | bytes 221188
  11.2 121.3 %all-to-all-start = ((bf16[12,3,256,128]{3,2,1,0:T(8,128)(2,1)}), bf16[12,3,256,128]{3,2,1,0:T(8,128)(2,1)S(1)}, u32[]{:S(2)}, u32[]{:S(2)}) async-start(bf16[12,3,256,128]{3,2,1,0:T(8,128)(2,1)} %broadcast_in_dim.76), calls=%async_computation | async-start | bytes 4718592 | tf_op jit(solution)/shard_map/all_to_all | solution.py:22
  22.6 103.1 %all-gather.3.cloned.1.call-start = ((), (), s32[]{:S(2)}) async-start(), calls=%async_computation.2 | async-start | bytes 3194880 | tf_op jit(solution)/shard_map/all_gather | solution.py:16
  132.5 1.9 copy-start.1
  132.7 3.4 copy-start.2
  139.6 275.3 %all-to-all-start.1 = ((bf16[12,3,256,128]{3,2,1,0:T(8,128)(2,1)}), bf16[12,3,256,128]{3,2,1,0:T(8,128)(2,1)}, u32[]{:S(2)}, u32[]{:S(2)}) async-start(bf16[12,3,256,128]{3,2,1,0:T(8,128)(2,1)} %maximum_bitcast_fusion), calls=%async_computation.1 | async-start | bytes 4718592 | tf_op jit(solution)/shard_map/all_to_all | solution.py:52
  146.3 1.1 copy-start.3
  146.3 53.1 %all-reduce.5.cloned.1.call-start = ((), (), s32[]{:S(2)}) async-start(), calls=%async_computation.3 | async-start | bytes 6291456
Sparse Core Ops, SparseCore 0:
  27.9 97.8 all-gather.2
  157.1 42.2 all-reduce.4
where the time goes:
time: 425 us
  blocking collectives  212 us (50%)
  waiting for transfers between devices  139 us (33%)
  local copies, waits for them, and re-layouts  26.4 us (6%)
  starting transfers between devices  18.2 us (4%)
  between operations  14.9 us (4%)
  other arithmetic  8.37 us (2%)
  matrix products  5.69 us (1%)
    unnamed x1, blocking collectives  212 us
    all_gather x1, waiting for transfers between devices, sent_together(): filled = lax.all_gather(both, axis, axis=dim, tiled=True)  100 us
    unnamed x3, waiting for transfers between devices  39.2 us
    unnamed x20, local copies, waits for them, and re-layouts  13.4 us
    all_to_all x1, starting transfers between devices, copy_for_each(): lax.all_to_all(jnp.broadcast_to(x[None], (length, *x.shape)), axis, 0, 0,...  11.4 us
  transfers between devices with their start and end apart: 4, of which 2 were waited for; matrix products, arithmetic and copies ran while one was open for 6% of the time, Pallas kernels for 0%

commit v1 on v0

v1 whole, which is shorter than its diff:
```python
import functools

import jax
import jax.numpy as jnp
from jax import lax
from jax.experimental import pallas as pl
from jax.experimental.pallas import tpu as pltpu
from jax.sharding import Mesh
from jax.sharding import PartitionSpec as P

TILE = 128
CAP = 3
PAD = 8
MESH = pl.DeviceIdType.MESH
AXES = ("x", "zl", "y", "zh", "core")
SIZES = (4, 3, 8, 4, 2)
F32 = jnp.float32
BF16 = jnp.bfloat16


def dot(left, right, contract=((1,), (0,))):
    return lax.dot_general(left, right, (contract, ((), ())), preferred_element_type=F32)


class Net:
    def __init__(self, send_sems, recv_sems):
        self.send_sems, self.recv_sems, self.copies = send_sems, recv_sems, []

    def send(self, src, dst, **where):
        i = len(self.copies)
        copy = pltpu.make_async_remote_copy(
            src_ref=src,
            dst_ref=dst,
            send_sem=self.send_sems.at[i],
            recv_sem=self.recv_sems.at[i],
            device_id=where,
            device_id_type=MESH,
        )
        copy.start()
        self.copies.append(copy)
        return copy


def kernel(
    sizes, og_ref, li_ref, ids_ref, prob_ref, w_ref, exp_ref, ig_ref, wg_ref,
    W, A, AR, HIT, Z, S, GU, HID, CX, CR, OWN, YS, YR, ZS, ZR, FR,
    G2, R2, G1, R1, GO, GS, GR, send_sems, recv_sems,
):
    nx, nz, ny, nh, _ = sizes
    x, zl, y, zh, core = (lax.axis_index(a) for a in AXES)
    d = li_ref.shape[1]
    half = d // 2
    rows, block = 6 * nh, w_ref.shape[1]
    net = Net(send_sems, recv_sems)

    def turn(at, by, n):
        return lax.rem(at + by + n, n)

    xs = {s: turn(x, s, nx) for s in (1, -1)}
    ys = {s: turn(y, s, ny) for s in (1, -1)}
    hs = {s: turn(zh, s, nh) for s in (1, -1)}
    other = 1 - core

    def piece(xx, zz):
        return pl.ds(pl.multiple_of((xx * nz + zz) * block, block), block)

    def halfpiece(xx, zz, part):
        size = block // 2
        return pl.ds(pl.multiple_of((xx * nz + zz) * block + part * size, size), size)

    for k in range(3):
        for t in range(block // TILE):
            e = exp_ref[t, :, k : k + 1]
            factor = jnp.where(e > 0, 2.0, jnp.where(e < 0, 0.5, 1.0)).astype(F32)
            scaled = (w_ref[k, t * TILE : (t + 1) * TILE, :].astype(F32) * factor).astype(BF16)
            at = pl.multiple_of((x * nz + zl) * block + t * TILE, TILE)
            W[pl.ds(at, TILE), k * TILE : (k + 1) * TILE] = scaled

    tokens = ids_ref.shape[1]
    r0, r1 = ids_ref[0:1, :] == 0, ids_ref[1:2, :] == 0
    routed = jnp.broadcast_to(jnp.where(r0 | r1, 1.0, 0.0).astype(F32), (PAD, tokens))
    prob = jnp.where(r0, prob_ref[0:1, :], 0.0) + jnp.where(r1, prob_ref[1:2, :], 0.0)
    upto = (
        lax.broadcasted_iota(jnp.int32, (tokens, tokens), 0)
        <= lax.broadcasted_iota(jnp.int32, (tokens, tokens), 1)
    )
    place = dot(routed.astype(BF16), jnp.where(upto, 1.0, 0.0).astype(BF16))
    wanted = (lax.broadcasted_iota(jnp.int32, (PAD, tokens), 0) - 3 * core + 1).astype(F32)
    hit = jnp.where(place == wanted, routed, 0.0)
    HIT[...] = hit
    hit_b = hit.astype(BF16)
    A[0] = dot(hit_b, li_ref[...]).astype(BF16)
    slot_prob = jnp.sum(hit * prob, axis=1, keepdims=True)
    A[1] = (slot_prob * dot(hit_b, og_ref[...])).astype(BF16)

    barrier = pltpu.get_barrier_semaphore()
    greeted = [dict(core=other)]
    if nx > 1:
        greeted += [dict(x=xs[1]), dict(x=xs[-1])]
    greeted += [dict(zl=turn(zl, s, nz)) for s in range(1, nz)]
    if ny > 1:
        greeted += [dict(y=ys[1]), dict(y=ys[-1])]
    if nh > 1:
        greeted += [dict(zh=hs[1]), dict(zh=hs[-1])]
    for where in greeted:
        pl.semaphore_signal(barrier, inc=1, device_id=where, device_id_type=MESH)
    pl.semaphore_wait(barrier, len(greeted))

    a_in = net.send(A.at[other], AR, core=other)
    own = W.at[piece(x, zl)]

    def spread(ref):
        return {s: net.send(ref, ref, x=xs[s]) for s in (1, -1)} if nx > 1 else None

    def relay(zz):
        if nx == 1:
            return None
        out = {}
        for s, part in ((1, 0), (-1, 1)):
            ref = W.at[halfpiece(xs[-s], zz, part)]
            out[s] = net.send(ref, ref, x=xs[s])
        return out

    def arrive(copies):
        for s in (1, -1):
            if copies is not None:
                copies[s].wait_recv()

    w_own = spread(own)
    w_z = [net.send(own, own, zl=turn(zl, s, nz)) for s in range(1, nz)]
    relays = []

    a_in.wait_recv()
    Z[zh] = A[core] + AR[...]
    z_in = {s: net.send(Z.at[zh], Z.at[zh], zh=hs[s]) for s in (1, -1)} if nh > 1 else None

    w_x = [(zl, w_own)]
    if nz > 1:
        w_z[0].wait_recv()
        zz = turn(zl, -1, nz)
        w_x.append((zz, spread(W.at[piece(x, zz)])))

    if nh > 1:
        arrive(z_in)
        z_far = []
        for s, part in ((1, 0), (-1, 1)):
            ref = Z.at[hs[-s], :, part * (half) : (part + 1) * half]
            z_far.append(net.send(ref, ref, zh=hs[s]))

    arrive(w_x[0][1])
    relays.append(relay(w_x[0][0]))
    if nz > 2:
        w_z[1].wait_recv()
        zz = turn(zl, -2, nz)
        w_x.append((zz, spread(W.at[piece(x, zz)])))

    if nh > 1:
        for copy in z_far:
            copy.wait_recv()

    packed = lax.broadcasted_iota(jnp.int32, (rows, nh * PAD), 0)
    padded = lax.broadcasted_iota(jnp.int32, (rows, nh * PAD), 1)
    same = padded == (packed // 6) * PAD + lax.rem(packed, 6)
    pack = jnp.where(same, 1.0, 0.0).astype(BF16)

    def yrows(yy):
        return pl.ds(pl.multiple_of(yy * rows, 8), rows)

    def ypart(yy, k):
        return S.at[core, yrows(yy), k * half : (k + 1) * half]

    S[core, yrows(y), :] = dot(pack, Z[...].reshape(nh * PAD, d)).astype(BF16)

    partner = []

    def to_partner(ref):
        partner.append(net.send(ref, ref, core=other))

    hops = ny // 2
    if ny > 1:
        y_in = {(s, k): net.send(ypart(y, k), ypart(y, k), y=ys[s]) for k in (0, 1) for s in (1, -1)}
    to_partner(S.at[core, yrows(y)])

    if nz > 1:
        arrive(w_x[1][1])
        relays.append(relay(w_x[1][0]))

    for hop in range(1, hops + 1):
        later = {}
        for k in (0, 1):
            for s in (1, -1):
                if (s, k) not in y_in:
                    continue
                y_in[s, k].wait_recv()
                ref = ypart(turn(y, -s * hop, ny), k)
                if hop < hops - 1 or (hop == hops - 1 and k == (0 if s == 1 else 1)):
                    later[s, k] = net.send(ref, ref, y=ys[s])
                to_partner(ref)
        y_in = later
        if hop == 1 and nz > 2:
            arrive(w_x[2][1])
            relays.append(relay(w_x[2][0]))

    for copies in relays:
        arrive(copies)
    for copy in partner:
        copy.wait_recv()

    total = rows * ny
    gate_up = dot(S[0, 0:total, :], W[:, 0 : 2 * TILE])
    back = dot(S[1, 0:total, :], W[:, 2 * TILE : 3 * TILE])
    gate, up = gate_up[:, 0:TILE], gate_up[:, TILE : 2 * TILE]
    sig = jax.nn.sigmoid(gate)
    act = gate * sig
    GU[:, 0:TILE] = (back * up * sig * (1.0 + gate * (1.0 - sig))).astype(BF16)
    GU[:, TILE : 2 * TILE] = (back * act).astype(BF16)
    HID[...] = (act * up).astype(BF16)

    step = block if half % block == 0 else TILE

    def back_part(which, put):
        for j in range(half // step):
            at = pl.multiple_of(which * half + j * step, step)
            put(j * step, dot(GU[...], W[pl.ds(at, step), 0 : 2 * TILE], ((1,), (1,))))

    def put_sent(at, value):
        CX[:, at : at + step] = value.astype(BF16)

    def put_own(at, value):
        OWN[:, at : at + step] = value

    def grads(xx, zz):
        at = piece(xx, zz)
        return (
            dot(GU[...], S[0, 0:total, at], ((0,), (0,))),
            dot(HID[...], S[1, 0:total, at], ((0,), (0,))),
        )

    gu_rows, all_rows = 2 * TILE, 3 * TILE
    mid = all_rows // 2

    back_part(other, put_sent)
    c_in = net.send(CX, CR, core=other)

    order = [turn(zl, s, nz) for s in range(1, nz)] + [zl]
    g2_in = []
    if nx > 1:
        for i, zz in enumerate(order):
            first, second = grads(turn(x, 2, nx), zz)
            G2[i, 0:gu_rows, :] = first.astype(BF16)
            G2[i, gu_rows:all_rows, :] = second.astype(BF16)
            g2_in.append(
                {
                    s: net.send(G2.at[i, part * mid : (part + 1) * mid], R2.at[part, i], x=xs[s])
                    for s, part in ((1, 0), (-1, 1))
                }
            )

    back_part(core, put_own)
    c_in.wait_recv()
    OWN[...] += CR[...].astype(F32)

    g1_in = []

    def send_near(i):
        if nx == 1:
            return
        arrive(g2_in[i])
        copies = {}
        for s, part in ((1, 0), (-1, 1)):
            first, second = grads(xs[s], order[i])
            G = jnp.concatenate([first, second], axis=0)
            lo, hi = part * mid, (part + 1) * mid
            G1[part, i, lo:hi, :] = (G[lo:hi] + R2[part, i].astype(F32)).astype(BF16)
            lo, hi = (1 - part) * mid, (2 - part) * mid
            G1[part, i, lo:hi, :] = G[lo:hi].astype(BF16)
            copies[s] = net.send(G1.at[part, i], R1.at[part, i], x=xs[s])
        g1_in.append(copies)

    def summed_here(i):
        first, second = grads(x, order[i])
        GO[0:gu_rows, :] = first
        GO[gu_rows:all_rows, :] = second
        if nx > 1:
            arrive(g1_in[i])
            GO[...] += R1[0, i].astype(F32) + R1[1, i].astype(F32)

    quarter = half // 2
    y_in = {}

    def y_step(hop):
        far = hops + 1 - hop
        copies = {}
        for s, part in ((1, 0), (-1, 1)):
            dest = yrows(turn(y, s * far, ny))
            mine = slice(part * quarter, (part + 1) * quarter)
            if hop == 1:
                YS[part, 0, :, mine] = OWN[dest, mine].astype(BF16)
                copies[s] = net.send(YS.at[part, 0, :, mine], YR.at[part, 0, :, mine], y=ys[s])
                continue
            y_in[s].wait_recv()
            if hop == 2:
                theirs = slice((1 - part) * quarter, (2 - part) * quarter)
                value = OWN[dest, mine] + YR[part, 0, :, mine].astype(F32)
                YS[part, 1, :, mine] = value.astype(BF16)
                YS[part, 1, :, theirs] = OWN[dest, theirs].astype(BF16)
            else:
                value = OWN[dest, :] + YR[part, hop - 2].astype(F32)
                YS[part, hop - 1] = value.astype(BF16)
            copies[s] = net.send(YS.at[part, hop - 1], YR.at[part, hop - 1], y=ys[s])
        y_in.update(copies)

    if ny > 1:
        y_step(1)
    for i in range(nz):
        send_near(i)
        if ny > 1 and i + 2 <= hops:
            y_step(i + 2)
    for hop in range(nz + 2, hops + 1):
        y_step(hop)

    gz_in = []

    def to_zl(i):
        summed_here(i)
        GS[i] = GO[...].astype(BF16)
        gz_in.append(net.send(GS.at[i], GR.at[i], zl=order[i]))

    if nz > 1:
        to_zl(0)

    mine_y = OWN[yrows(y), :]
    if ny > 1:
        for s, part in ((1, 0), (-1, 1)):
            y_in[s].wait_recv()
            mine_y = mine_y + YR[part, hops - 1].astype(F32)
    spread_rows = dot(pack, mine_y.astype(BF16), ((0,), (0,)))
    ZS[...] = spread_rows.reshape(nh, PAD, half).astype(BF16)

    def zpart(part):
        return slice(part * quarter, (part + 1) * quarter)

    if nh > 1:
        far = turn(zh, 2, nh)
        z_in = {
            s: net.send(ZS.at[far, :, zpart(part)], ZR.at[part, 0, :, zpart(part)], zh=hs[s])
            for s, part in ((1, 0), (-1, 1))
        }
    if nz > 2:
        to_zl(1)
    if nh > 1:
        nearer = {}
        for s, part in ((1, 0), (-1, 1)):
            z_in[s].wait_recv()
            mine, theirs = zpart(part), zpart(1 - part)
            value = ZS[hs[s], :, mine].astype(F32) + ZR[part, 0, :, mine].astype(F32)
            ZR[part, 1, :, mine] = value.astype(BF16)
            ZR[part, 1, :, theirs] = ZS[hs[s], :, theirs]
            nearer[s] = net.send(ZR.at[part, 1], ZR.at[part, 2], zh=hs[s])

    summed_here(nz - 1)

    final = ZS[zh].astype(F32)
    if nh > 1:
        for s, part in ((1, 0), (-1, 1)):
            nearer[s].wait_recv()
            final = final + ZR[part, 2].astype(F32)
    FR[core] = final.astype(BF16)
    f_in = net.send(FR.at[core], FR.at[core], core=other)

    for i, copy in enumerate(gz_in):
        copy.wait_recv()
        GO[...] += GR[i].astype(F32)
    for k in range(3):
        wg_ref[k] = GO[k * TILE : (k + 1) * TILE, :].T

    f_in.wait_recv()
    hit_b = HIT[...].astype(BF16)
    for c in (0, 1):
        ig_ref[:, c * half : (c + 1) * half] = dot(hit_b, FR[c], ((0,), (0,))).astype(BF16)

    for copy in net.copies:
        copy.wait_send()


def per_device(sizes, out_grad, layer_input, expert_ids, gate_prob, w_stack, scale_exps):
    nx, nz, ny, nh, _ = sizes
    tokens, d = layer_input.shape
    block = w_stack.shape[1]
    half, rows, wide = d // 2, 6 * nh, 3 * TILE
    total = rows * ny
    hops = max(ny // 2, 1)
    held = total + 8 if total % 16 == 0 else total
    vmem = pl.BlockSpec(memory_space=pltpu.VMEM)
    scratch = [
        pltpu.VMEM((d, wide), BF16),
        pltpu.VMEM((2, PAD, d), BF16),
        pltpu.VMEM((PAD, d), BF16),
        pltpu.VMEM((PAD, tokens), F32),
        pltpu.VMEM((nh, PAD, d), BF16),
        pltpu.VMEM((2, held, d), BF16),
        pltpu.VMEM((total, 2 * TILE), BF16),
        pltpu.VMEM((total, TILE), BF16),
        pltpu.VMEM((total, half), BF16),
        pltpu.VMEM((total, half), BF16),
        pltpu.VMEM((total, half), F32),
        pltpu.VMEM((2, hops, rows, half), BF16),
        pltpu.VMEM((2, hops, rows, half), BF16),
        pltpu.VMEM((nh, PAD, half), BF16),
        pltpu.VMEM((2, 3, PAD, half), BF16),
        pltpu.VMEM((2, PAD, half), BF16),
        pltpu.VMEM((nz, wide, block), BF16),
        pltpu.VMEM((2, nz, wide // 2, block), BF16),
        pltpu.VMEM((2, nz, wide, block), BF16),
        pltpu.VMEM((2, nz, wide, block), BF16),
        pltpu.VMEM((wide, block), F32),
        pltpu.VMEM((nz, wide, block), BF16),
        pltpu.VMEM((nz, wide, block), BF16),
        pltpu.SemaphoreType.DMA((96,)),
        pltpu.SemaphoreType.DMA((96,)),
    ]
    return pl.pallas_call(
        functools.partial(kernel, sizes),
        out_shape=(
            jax.ShapeDtypeStruct((tokens, d), BF16),
            jax.ShapeDtypeStruct(w_stack.shape, F32),
        ),
        in_specs=[vmem] * 6,
        out_specs=(vmem, vmem),
        scratch_shapes=scratch,
        compiler_params=pltpu.CompilerParams(
            collective_id=0, has_side_effects=True, vmem_limit_bytes=48 * 1024 * 1024
        ),
        name="expert_backward",
    )(
        out_grad,
        layer_input,
        expert_ids.T,
        gate_prob.T,
        w_stack,
        jnp.transpose(scale_exps, (1, 2, 0)),
    )


def build(devices, sizes):
    split = Mesh(devices.reshape(sizes), AXES)
    tokens = P(AXES, None)
    weights = P(None, ("x", "zl"), ("y", "zh", "core"))
    return jax.shard_map(
        functools.partial(per_device, sizes),
        mesh=split,
        in_specs=(tokens, tokens, tokens, tokens, weights, weights),
        out_specs=(tokens, weights),
        check_vma=False,
    )


def solution(mesh):
    return build(mesh.devices, SIZES)
```

time: 425 us -> 95.6 us (0.22)
  the two profiles are of different devices: /device:TPU:128 before, /device:TPU:73 now
where the time goes in v1:
time: 95.6 us; the launch traced here: 95.4 us
  Pallas kernels  89.9 us (94%)
  local copies, waits for them, and re-layouts  4.79 us (5%)
    pallas_call x1, Pallas kernels, per_device(): pl.pallas_call(functools.partial(kernel, sizes), out_shape=(jax.ShapeDtyp...  89.9 us
    unnamed x14, local copies, waits for them, and re-layouts  4.79 us

profile of v1, /device:TPU:73, one launch (start us, length us, event | category | flops | bytes accessed | tf_op | source)
XLA Modules:
  0.0 95.4 jit_solution(8478477575712171906)
XLA Ops:
  0.6 0.0 copy-start.4
  0.6 0.0 copy-start.5
  0.7 0.0 copy-start.3
  0.7 0.7 copy-done.4
  1.3 0.0 copy-done.5
  1.3 0.0 copy-done.3
  1.3 0.0 copy-start
  1.3 0.9 copy-done
  2.3 0.0 copy-start.1
  2.3 0.9 copy-done.1
  3.2 0.0 copy-start.2
  3.2 0.9 copy-done.2
  4.1 89.9 %expert_backward.1 = (bf16[12,3072]{1,0:T(8,128)(2,1)S(1)}, f32[3,256,128]{2,1,0:T(8,128)S(1)}) custom-call(bf16[12,3072]{1,0:T(8,128)(2,1)S(1)} %copy-done.1, bf16[12,3072]{1,0:T(8,128)(2,1)S(1)} %copy-done.2, s32[2,12]{1,0:T(2,128)S(1)} %bitcast.3, f32[2,12]{1,0:T(2,128)S(1)} %bitcast.4, bf16[3,256,128]{2,1,0:T(8,128)(2,1)S(1)} %copy-done, ...), custom_call_target="tpu_custom_call" | custom-call | tf_op jit(solution)/shard_map/expert_backward/pallas_call | solution.py:422
  94.0 0.6 copy.10
  94.6 0.7 copy.11
Async XLA Ops:
  0.6 0.7 copy-start.4
  0.6 0.7 copy-start.5
  0.7 0.7 copy-start.3
  1.3 0.9 copy-start
  2.3 0.9 copy-start.1
  3.2 0.9 copy-start.2

commit v2 on v1

v2 whole, which is shorter than its diff:
```python
import functools

import jax
import jax.numpy as jnp
from jax import lax
from jax.experimental import pallas as pl
from jax.experimental.pallas import tpu as pltpu
from jax.sharding import Mesh
from jax.sharding import PartitionSpec as P

TILE = 128
CAP = 3
PAD = 8
MESH = pl.DeviceIdType.MESH
AXES = ("x", "zl", "y", "zh", "core")
SIZES = (4, 3, 8, 4, 2)
F32 = jnp.float32
BF16 = jnp.bfloat16


def dot(left, right, contract=((1,), (0,))):
    return lax.dot_general(left, right, (contract, ((), ())), preferred_element_type=F32)


class Net:
    def __init__(self, send_sems, recv_sems):
        self.send_sems, self.recv_sems, self.copies = send_sems, recv_sems, []

    def send(self, src, dst, **where):
        i = len(self.copies)
        copy = pltpu.make_async_remote_copy(
            src_ref=src,
            dst_ref=dst,
            send_sem=self.send_sems.at[i],
            recv_sem=self.recv_sems.at[i],
            device_id=where,
            device_id_type=MESH,
        )
        copy.start()
        self.copies.append(copy)
        return copy


def kernel(
    sizes, og_hbm, li_hbm, ids_hbm, prob_hbm, w_hbm, exp_hbm, ig_ref, wg_ref,
    og_ref, li_ref, ids_ref, prob_ref, w_ref, exp_ref,
    W, A, AR, HIT, Z, S, GU, GT, HT, CX, CR, OWN, YS, YR, ZS, ZR, FR,
    G2, R2, G1, R1, GO, GS, GR, send_sems, recv_sems, load_sems, known,
):
    nx, nz, ny, nh, _ = sizes
    x, zl, y, zh, core = (lax.axis_index(a) for a in AXES)
    d = li_ref.shape[1]
    half = d // 2
    rows, block = 6 * nh, w_ref.shape[1]
    hops = ny // 2
    net = Net(send_sems, recv_sems)

    def turn(at, by, n):
        return lax.rem(at + by + n, n)

    xs = {s: turn(x, s, nx) for s in (1, -1)}
    ys = {s: turn(y, s, ny) for s in (1, -1)}
    hs = {s: turn(zh, s, nh) for s in (1, -1)}
    other = 1 - core

    barrier = pltpu.get_barrier_semaphore()
    greeted = [dict(core=other)]
    if nx > 1:
        greeted += [dict(x=xs[1]), dict(x=xs[-1])]
    greeted += [dict(zl=turn(zl, s, nz)) for s in range(1, nz)]
    if ny > 1:
        greeted += [dict(y=ys[1]), dict(y=ys[-1])]
    if nh > 1:
        greeted += [dict(zh=hs[1]), dict(zh=hs[-1])]
    for where in greeted:
        pl.semaphore_signal(barrier, inc=1, device_id=where, device_id_type=MESH)

    pairs = [
        (w_hbm, w_ref), (exp_hbm, exp_ref), (ids_hbm, ids_ref), (prob_hbm, prob_ref),
        (li_hbm, li_ref), (og_hbm, og_ref),
    ]
    loads = [pltpu.make_async_copy(src, dst, load_sems.at[i]) for i, (src, dst) in enumerate(pairs)]
    for load in loads:
        load.start()

    def piece(xx, zz):
        return pl.ds(pl.multiple_of((xx * nz + zz) * block, block), block)

    def halfpiece(xx, zz, part):
        size = block // 2
        return pl.ds(pl.multiple_of((xx * nz + zz) * block + part * size, size), size)

    def got(copy, name):
        with jax.named_scope(name):
            copy.wait_recv()

    def arrive(copies, name):
        for s in (1, -1):
            if copies is not None:
                got(copies[s], name)

    for load in loads[2:]:
        load.wait()
    tokens = ids_ref.shape[1]
    r0, r1 = ids_ref[0:1, :] == 0, ids_ref[1:2, :] == 0
    routed = jnp.broadcast_to(jnp.where(r0 | r1, 1.0, 0.0).astype(F32), (PAD, tokens))
    prob = jnp.where(r0, prob_ref[0:1, :], 0.0) + jnp.where(r1, prob_ref[1:2, :], 0.0)
    upto = (
        lax.broadcasted_iota(jnp.int32, (tokens, tokens), 0)
        <= lax.broadcasted_iota(jnp.int32, (tokens, tokens), 1)
    )
    place = dot(routed.astype(BF16), jnp.where(upto, 1.0, 0.0).astype(BF16))
    wanted = (lax.broadcasted_iota(jnp.int32, (PAD, tokens), 0) - 3 * core + 1).astype(F32)
    hit = jnp.where(place == wanted, routed, 0.0)
    HIT[...] = hit
    hit_b = hit.astype(BF16)
    A[0] = dot(hit_b, li_ref[...]).astype(BF16)
    slot_prob = jnp.sum(hit * prob, axis=1, keepdims=True)
    A[1] = (slot_prob * dot(hit_b, og_ref[...])).astype(BF16)

    for load in loads[:2]:
        load.wait()
    for k in range(3):
        for t in range(block // TILE):
            e = exp_ref[t, :, k : k + 1]
            factor = jnp.where(e > 0, 2.0, jnp.where(e < 0, 0.5, 1.0)).astype(F32)
            scaled = (w_ref[k, t * TILE : (t + 1) * TILE, :].astype(F32) * factor).astype(BF16)
            at = pl.multiple_of((x * nz + zl) * block + t * TILE, TILE)
            W[pl.ds(at, TILE), k * TILE : (k + 1) * TILE] = scaled

    with jax.named_scope("greet"):
        pl.semaphore_wait(barrier, len(greeted))
    if nh > 1:
        for s in (1, -1):
            pl.semaphore_signal(known, inc=1, device_id=dict(zh=hs[s]), device_id_type=MESH)

    a_in = net.send(A.at[other], AR, core=other)
    own = W.at[piece(x, zl)]

    def spread(ref):
        return {s: net.send(ref, ref, x=xs[s]) for s in (1, -1)} if nx > 1 else None

    def relay(zz):
        if nx == 1:
            return None
        out = {}
        for s, part in ((1, 0), (-1, 1)):
            ref = W.at[halfpiece(xs[-s], zz, part)]
            out[s] = net.send(ref, ref, x=xs[s])
        return out

    w_x = [(zl, spread(own))]
    relays = []

    got(a_in, "a")
    Z[zh] = A[core] + AR[...]
    if nh > 1:
        z_in = {s: net.send(Z.at[zh], Z.at[zh], zh=hs[s]) for s in (1, -1)}
    w_z = []
    if nz > 1:
        w_z.append(net.send(own, own, zl=turn(zl, 1, nz)))
    if nh > 1:
        arrive(z_in, "zh")
        z_far = []
        for s, part in ((1, 0), (-1, 1)):
            ref = Z.at[hs[-s], :, part * half : (part + 1) * half]
            z_far.append(net.send(ref, ref, zh=hs[s]))
    if nz > 2:
        w_z.append(net.send(own, own, zl=turn(zl, 2, nz)))

    arrive(w_x[0][1], "wx0")
    relays.append(relay(w_x[0][0]))
    if nz > 1:
        got(w_z[0], "wz0")
        zz = turn(zl, -1, nz)
        w_x.append((zz, spread(W.at[piece(x, zz)])))

    if nh > 1:
        for copy in z_far:
            got(copy, "zfar")

    packed = lax.broadcasted_iota(jnp.int32, (rows, nh * PAD), 0)
    padded = lax.broadcasted_iota(jnp.int32, (rows, nh * PAD), 1)
    same = padded == (packed // 6) * PAD + lax.rem(packed, 6)
    pack = jnp.where(same, 1.0, 0.0).astype(BF16)

    def yrows(yy):
        return pl.ds(pl.multiple_of(yy * rows, 8), rows)

    def ypart(yy, k):
        return S.at[core, yrows(yy), k * half : (k + 1) * half]

    S[core, yrows(y), :] = dot(pack, Z[...].reshape(nh * PAD, d)).astype(BF16)

    partner = []

    def to_partner(ref):
        partner.append(net.send(ref, ref, core=other))

    if ny > 1:
        y_in = {(s, k): net.send(ypart(y, k), ypart(y, k), y=ys[s]) for k in (0, 1) for s in (1, -1)}
    to_partner(S.at[core, yrows(y)])

    if nz > 2:
        got(w_z[1], "wz1")
        zz = turn(zl, -2, nz)
        w_x.append((zz, spread(W.at[piece(x, zz)])))

    def relay_next():
        at = len(relays)
        if at < nz:
            arrive(w_x[at][1], f"wx{at}")
            relays.append(relay(w_x[at][0]))

    for hop in range(1, hops + 1):
        later = {}
        for k in (0, 1):
            for s in (1, -1):
                if (s, k) not in y_in:
                    continue
                got(y_in[s, k], f"y{hop}")
                ref = ypart(turn(y, -s * hop, ny), k)
                if hop < hops - 1 or (hop == hops - 1 and k == (0 if s == 1 else 1)):
                    later[s, k] = net.send(ref, ref, y=ys[s])
                to_partner(ref)
        y_in = later
        relay_next()
    for _ in range(nz):
        relay_next()

    for copies in relays:
        arrive(copies, "wfar")
    for copy in partner:
        got(copy, "partner")

    total = rows * ny
    gate_up = dot(S[0, 0:total, :], W[:, 0 : 2 * TILE])
    back = dot(S[1, 0:total, :], W[:, 2 * TILE : 3 * TILE])
    gate, up = gate_up[:, 0:TILE], gate_up[:, TILE : 2 * TILE]
    sig = jax.nn.sigmoid(gate)
    act = gate * sig
    gate_grad = back * up * sig * (1.0 + gate * (1.0 - sig))
    up_grad = back * act
    GU[:, 0:TILE] = gate_grad.astype(BF16)
    GU[:, TILE : 2 * TILE] = up_grad.astype(BF16)
    GT[0:TILE, :] = gate_grad.T.astype(BF16)
    GT[TILE : 2 * TILE, :] = up_grad.T.astype(BF16)
    HT[...] = (act * up).T.astype(BF16)

    step = block if half % block == 0 else TILE

    def back_part(which, put):
        for j in range(half // step):
            at = pl.multiple_of(which * half + j * step, step)
            put(j * step, dot(GU[...], W[pl.ds(at, step), 0 : 2 * TILE], ((1,), (1,))))

    def put_sent(at, value):
        CX[:, at : at + step] = value.astype(BF16)

    def put_own(at, value):
        OWN[:, at : at + step] = value

    def grads(xx, zz):
        at = piece(xx, zz)
        return dot(GT[...], S[0, 0:total, at]), dot(HT[...], S[1, 0:total, at])

    gu_rows, all_rows = 2 * TILE, 3 * TILE
    mid = all_rows // 2
    order = [turn(zl, s, nz) for s in range(1, nz)] + [zl]
    g2_in, g1_in, gz_in = {}, {}, []

    def send_far(i):
        if nx == 1:
            return
        first, second = grads(turn(x, 2, nx), order[i])
        G2[i, 0:gu_rows, :] = first.astype(BF16)
        G2[i, gu_rows:all_rows, :] = second.astype(BF16)
        g2_in[i] = {
            s: net.send(G2.at[i, part * mid : (part + 1) * mid], R2.at[part, i], x=xs[s])
            for s, part in ((1, 0), (-1, 1))
        }

    def send_near(i):
        if nx == 1:
            return
        arrive(g2_in[i], f"g2_{i}")
        copies = {}
        for s, part in ((1, 0), (-1, 1)):
            first, second = grads(xs[s], order[i])
            G = jnp.concatenate([first, second], axis=0)
            lo, hi = part * mid, (part + 1) * mid
            G1[part, i, lo:hi, :] = (G[lo:hi] + R2[part, i].astype(F32)).astype(BF16)
            lo, hi = (1 - part) * mid, (2 - part) * mid
            G1[part, i, lo:hi, :] = G[lo:hi].astype(BF16)
            copies[s] = net.send(G1.at[part, i], R1.at[part, i], x=xs[s])
        g1_in[i] = copies

    def summed_here(i):
        first, second = grads(x, order[i])
        GO[0:gu_rows, :] = first
        GO[gu_rows:all_rows, :] = second
        if nx > 1:
            arrive(g1_in[i], f"g1_{i}")
            GO[...] += R1[0, i].astype(F32) + R1[1, i].astype(F32)

    def to_zl(i):
        if i < nz - 1:
            summed_here(i)
            GS[i] = GO[...].astype(BF16)
            gz_in.append(net.send(GS.at[i], GR.at[i], zl=order[i]))

    quarter = half // 2
    quarters = [slice(q * quarter, (q + 1) * quarter) for q in (0, 1)]
    y_in = {}

    def y_step(t):
        for kind in (0, 1):
            for s, part in ((1, 0), (-1, 1)):
                far = hops + 1 - t - kind
                if far < 1:
                    continue
                q = quarters[part if kind == 0 else 1 - part]
                value = OWN[yrows(turn(y, s * far, ny)), q]
                if t > 1:
                    got(y_in[kind, s], f"r{t}")
                    value = value + YR[part, kind, t - 2].astype(F32)
                YS[part, kind, t - 1] = value.astype(BF16)
                y_in[kind, s] = net.send(
                    YS.at[part, kind, t - 1], YR.at[part, kind, t - 1], y=ys[s]
                )

    send_far(0)
    back_part(other, put_sent)
    c_in = net.send(CX, CR, core=other)
    if nz > 1:
        send_far(1)
    back_part(core, put_own)
    got(c_in, "c")
    OWN[...] += CR[...].astype(F32)
    if hops > 0:
        y_step(1)
    send_near(0)
    if nz > 2:
        send_far(2)
    if hops > 1:
        y_step(2)
    if nz > 1:
        send_near(1)
    if hops > 2:
        y_step(3)
    to_zl(0)
    if hops > 3:
        y_step(4)
    if nz > 2:
        send_near(2)

    mine_y = [OWN[yrows(y), q] for q in quarters]
    for kind in (0, 1):
        for s, part in ((1, 0), (-1, 1)):
            if hops > kind:
                got(y_in[kind, s], "rlast")
                q = part if kind == 0 else 1 - part
                mine_y[q] = mine_y[q] + YR[part, kind, hops - 1 - kind].astype(F32)
    for q in (0, 1):
        spread_rows = dot(pack, mine_y[q].astype(BF16), ((0,), (0,)))
        ZS[:, :, quarters[q]] = spread_rows.reshape(nh, PAD, quarter).astype(BF16)

    if nh > 1:
        pl.semaphore_wait(known, 2)
        z_in = []
        for i, s in enumerate((2, 1, -1)):
            there = turn(zh, s, nh)
            z_in.append(net.send(ZS.at[there], ZR.at[i], zh=there))
    to_zl(1)

    final = ZS[zh].astype(F32)
    if nh > 1:
        for i in (1, 2, 0):
            got(z_in[i], f"rz{i}")
        for i in range(3):
            final = final + ZR[i].astype(F32)
    FR[core] = final.astype(BF16)
    f_in = net.send(FR.at[core], FR.at[core], core=other)

    summed_here(nz - 1)
    for i, copy in enumerate(gz_in):
        got(copy, f"gz{i}")
        GO[...] += GR[i].astype(F32)
    for k in range(3):
        wg_ref[k] = GO[k * TILE : (k + 1) * TILE, :].T

    got(f_in, "f")
    hit_b = HIT[...].astype(BF16)
    for c in (0, 1):
        ig_ref[:, c * half : (c + 1) * half] = dot(hit_b, FR[c], ((0,), (0,))).astype(BF16)

    for copy in net.copies:
        copy.wait_send()


def per_device(sizes, out_grad, layer_input, expert_ids, gate_prob, w_stack, scale_exps):
    nx, nz, ny, nh, _ = sizes
    tokens, d = layer_input.shape
    block = w_stack.shape[1]
    half, rows, wide = d // 2, 6 * nh, 3 * TILE
    total = rows * ny
    hops = max(ny // 2, 1)
    held = total + 8 if total % 16 == 0 else total
    vmem = pl.BlockSpec(memory_space=pltpu.VMEM)
    arrays = (
        out_grad,
        layer_input,
        expert_ids.T,
        gate_prob.T,
        w_stack,
        jnp.transpose(scale_exps, (1, 2, 0)),
    )
    scratch = [pltpu.VMEM(a.shape, a.dtype) for a in arrays] + [
        pltpu.VMEM((d, wide), BF16),
        pltpu.VMEM((2, PAD, d), BF16),
        pltpu.VMEM((PAD, d), BF16),
        pltpu.VMEM((PAD, tokens), F32),
        pltpu.VMEM((nh, PAD, d), BF16),
        pltpu.VMEM((2, held, d), BF16),
        pltpu.VMEM((total, 2 * TILE), BF16),
        pltpu.VMEM((2 * TILE, total), BF16),
        pltpu.VMEM((TILE, total), BF16),
        pltpu.VMEM((total, half), BF16),
        pltpu.VMEM((total, half), BF16),
        pltpu.VMEM((total, half), F32),
        pltpu.VMEM((2, 2, hops, rows, half // 2), BF16),
        pltpu.VMEM((2, 2, hops, rows, half // 2), BF16),
        pltpu.VMEM((nh, PAD, half), BF16),
        pltpu.VMEM((3, PAD, half), BF16),
        pltpu.VMEM((2, PAD, half), BF16),
        pltpu.VMEM((nz, wide, block), BF16),
        pltpu.VMEM((2, nz, wide // 2, block), BF16),
        pltpu.VMEM((2, nz, wide, block), BF16),
        pltpu.VMEM((2, nz, wide, block), BF16),
        pltpu.VMEM((wide, block), F32),
        pltpu.VMEM((nz, wide, block), BF16),
        pltpu.VMEM((nz, wide, block), BF16),
        pltpu.SemaphoreType.DMA((96,)),
        pltpu.SemaphoreType.DMA((96,)),
        pltpu.SemaphoreType.DMA((6,)),
        pltpu.SemaphoreType.REGULAR,
    ]
    return pl.pallas_call(
        functools.partial(kernel, sizes),
        out_shape=(
            jax.ShapeDtypeStruct((tokens, d), BF16),
            jax.ShapeDtypeStruct(w_stack.shape, F32),
        ),
        in_specs=[pl.BlockSpec(memory_space=pltpu.HBM)] * 6,
        out_specs=(vmem, vmem),
        scratch_shapes=scratch,
        compiler_params=pltpu.CompilerParams(
            collective_id=0, has_side_effects=True, vmem_limit_bytes=67043328
        ),
        name="expert_backward",
    )(*arrays)


def build(devices, sizes):
    split = Mesh(devices.reshape(sizes), AXES)
    tokens = P(AXES, None)
    weights = P(None, ("x", "zl"), ("y", "zh", "core"))
    return jax.shard_map(
        functools.partial(per_device, sizes),
        mesh=split,
        in_specs=(tokens, tokens, tokens, tokens, weights, weights),
        out_specs=(tokens, weights),
        check_vma=False,
    )


def solution(mesh):
    return build(mesh.devices, SIZES)
```

time: 95.6 us -> 83.5 us (0.87)
  the two profiles are of different devices: /device:TPU:73 before, /device:TPU:1 now
where the time goes in v2:
time: 83.5 us; the launch traced here: 83.2 us
  Pallas kernels  79.3 us (95%)
  local copies, waits for them, and re-layouts  3.31 us (4%)
    pallas_call x1, Pallas kernels, per_device(): pl.pallas_call(functools.partial(kernel, sizes), out_shape=(jax.ShapeDtyp...  79.3 us
    unnamed x2, local copies, waits for them, and re-layouts  3.31 us

profile of v2, /device:TPU:1, one launch (start us, length us, event | category | flops | bytes accessed | tf_op | source)
XLA Modules:
  0.0 83.2 jit_solution(17524248682446265025)
XLA Ops:
  0.6 79.3 %expert_backward.1 = (bf16[12,3072]{1,0:T(8,128)(2,1)}, f32[3,256,128]{2,1,0:T(8,128)}) custom-call(bf16[12,3072]{1,0:T(8,128)(2,1)} %og_hbm.1, bf16[12,3072]{1,0:T(8,128)(2,1)} %li_hbm.1, s32[2,12]{1,0:T(2,128)} %bitcast.3, f32[2,12]{1,0:T(2,128)} %bitcast.4, bf16[3,256,128]{2,1,0:T(8,128)(2,1)} %w_hbm.1, s32[2,1,3]{2,1,0:T(1,128)} %bitcast.5), custom_call_target="tpu_custom_call" | custom-call | tf_op jit(solution)/shard_map/expert_backward/pallas_call | solution.py:448
  79.9 1.5 %copy.10 = bf16[12,3072]{1,0:T(8,128)(2,1)} copy(bf16[12,3072]{1,0:T(8,128)(2,1)} %get-tuple-element.4) | data formatting | bytes 147456
  81.5 1.8 %copy.11 = f32[3,256,128]{2,1,0:T(8,128)} copy(f32[3,256,128]{2,1,0:T(8,128)} %get-tuple-element.5) | data formatting | bytes 786432

commit v3 on v2

v3 whole, which is shorter than its diff:
```python
import functools

import jax
import jax.numpy as jnp
from jax import lax
from jax.experimental import pallas as pl
from jax.experimental.pallas import tpu as pltpu
from jax.sharding import Mesh
from jax.sharding import PartitionSpec as P

TILE = 128
CAP = 3
PAD = 8
MESH = pl.DeviceIdType.MESH
AXES = ("x", "zl", "y", "zh", "core")
SIZES = (4, 3, 8, 4, 2)
F32 = jnp.float32
BF16 = jnp.bfloat16


def dot(left, right, contract=((1,), (0,))):
    return lax.dot_general(left, right, (contract, ((), ())), preferred_element_type=F32)


class Net:
    def __init__(self, send_sems, recv_sems):
        self.send_sems, self.recv_sems, self.copies = send_sems, recv_sems, []

    def send(self, src, dst, **where):
        i = len(self.copies)
        copy = pltpu.make_async_remote_copy(
            src_ref=src,
            dst_ref=dst,
            send_sem=self.send_sems.at[i],
            recv_sem=self.recv_sems.at[i],
            device_id=where,
            device_id_type=MESH,
        )
        copy.start()
        self.copies.append(copy)
        return copy


def kernel(
    sizes, og_hbm, li_hbm, ids_hbm, prob_hbm, w_hbm, exp_hbm, ig_ref, wg_ref,
    og_ref, li_ref, ids_ref, prob_ref, w_ref, exp_ref,
    W, A, AR, HIT, S, GU, GP, GT, HT, CX, CR, OWN, YS, YR, ZS, ZR, FR,
    G2, R2, G1, R1, GO, GS, GR, DS, DR, DG, D2, E2, D1, E1,
    send_sems, recv_sems, load_sems, known,
):
    nx, nz, ny, nh, _ = sizes
    x, zl, y, zh, core = (lax.axis_index(a) for a in AXES)
    d = li_ref.shape[1]
    half = d // 2
    rows, block = PAD * nh, w_ref.shape[1]
    total = rows * ny
    hops = ny // 2
    net = Net(send_sems, recv_sems)

    def turn(at, by, n):
        return lax.rem(at + by + n, n)

    xs = {s: turn(x, s, nx) for s in (1, -1)}
    ys = {s: turn(y, s, ny) for s in (1, -1)}
    hs = {s: turn(zh, s, nh) for s in (1, -1)}
    other = 1 - core
    both = ((1, 0), (-1, 1))

    barrier = pltpu.get_barrier_semaphore()
    greeted = [dict(core=other)]
    if nx > 1:
        greeted += [dict(x=xs[1]), dict(x=xs[-1])]
    greeted += [dict(zl=turn(zl, s, nz)) for s in range(1, nz)]
    if ny > 1:
        greeted += [dict(y=ys[1]), dict(y=ys[-1])]
    if nh > 1:
        greeted += [dict(zh=hs[1]), dict(zh=hs[-1])]
    for where in greeted:
        pl.semaphore_signal(barrier, inc=1, device_id=where, device_id_type=MESH)

    pairs = [
        (w_hbm, w_ref), (exp_hbm, exp_ref), (ids_hbm, ids_ref), (prob_hbm, prob_ref),
        (li_hbm, li_ref), (og_hbm, og_ref),
    ]
    loads = [pltpu.make_async_copy(src, dst, load_sems.at[i]) for i, (src, dst) in enumerate(pairs)]
    for load in loads:
        load.start()

    def piece(xx, zz):
        return pl.ds(pl.multiple_of((xx * nz + zz) * block, block), block)

    def halfpiece(xx, zz, part):
        size = block // 2
        return pl.ds(pl.multiple_of((xx * nz + zz) * block + part * size, size), size)

    def got(copy, name):
        with jax.named_scope(name):
            copy.wait_recv()

    def arrive(copies, name):
        for s in (1, -1):
            if copies is not None:
                got(copies[s], name)

    for load in loads[2:]:
        load.wait()
    tokens = ids_ref.shape[1]
    r0, r1 = ids_ref[0:1, :] == 0, ids_ref[1:2, :] == 0
    routed = jnp.broadcast_to(jnp.where(r0 | r1, 1.0, 0.0).astype(F32), (PAD, tokens))
    prob = jnp.where(r0, prob_ref[0:1, :], 0.0) + jnp.where(r1, prob_ref[1:2, :], 0.0)
    upto = (
        lax.broadcasted_iota(jnp.int32, (tokens, tokens), 0)
        <= lax.broadcasted_iota(jnp.int32, (tokens, tokens), 1)
    )
    place = dot(routed.astype(BF16), jnp.where(upto, 1.0, 0.0).astype(BF16))
    wanted = (lax.broadcasted_iota(jnp.int32, (PAD, tokens), 0) - CAP * core + 1).astype(F32)
    hit = jnp.where(place == wanted, routed, 0.0)
    HIT[...] = hit
    hit_b = hit.astype(BF16)
    A[0] = dot(hit_b, li_ref[...]).astype(BF16)
    slot_prob = jnp.sum(hit * prob, axis=1, keepdims=True)
    A[1] = (slot_prob * dot(hit_b, og_ref[...])).astype(BF16)

    for load in loads[:2]:
        load.wait()
    for k in range(3):
        for t in range(block // TILE):
            e = exp_ref[t, :, k : k + 1]
            factor = jnp.where(e > 0, 2.0, jnp.where(e < 0, 0.5, 1.0)).astype(F32)
            scaled = (w_ref[k, t * TILE : (t + 1) * TILE, :].astype(F32) * factor).astype(BF16)
            at = pl.multiple_of((x * nz + zl) * block + t * TILE, TILE)
            W[pl.ds(at, TILE), k * TILE : (k + 1) * TILE] = scaled

    with jax.named_scope("greet"):
        pl.semaphore_wait(barrier, len(greeted))
    if nh > 1:
        for s in (1, -1):
            pl.semaphore_signal(known, inc=1, device_id=dict(zh=hs[s]), device_id_type=MESH)

    gu_lanes, all_lanes, down_lanes = slice(0, 2 * TILE), slice(0, 3 * TILE), slice(2 * TILE, 3 * TILE)
    a_in = net.send(A.at[other], AR, core=other)

    def spread(zz, lanes):
        if nx == 1:
            return None
        ref = W.at[piece(x, zz), lanes]
        return {s: net.send(ref, ref, x=xs[s]) for s in (1, -1)}

    def relay(zz, lanes):
        if nx == 1:
            return None
        out = {}
        for s, part in both:
            ref = W.at[halfpiece(xs[-s], zz, part), lanes]
            out[s] = net.send(ref, ref, x=xs[s])
        return out

    def own_to_zl(i):
        ref = W.at[piece(x, zl), all_lanes]
        return net.send(ref, ref, zl=turn(zl, i, nz))

    down_in = []

    def down_to_zl(rows_at):
        for i in range(1, nz):
            ref = W.at[rows_at, down_lanes]
            down_in.append(net.send(ref, ref, zl=turn(zl, i, nz)))

    def sub(yy, hh):
        return pl.ds(pl.multiple_of((yy * nh + hh) * PAD, PAD), PAD)

    def yrows(yy):
        return pl.ds(pl.multiple_of(yy * rows, rows), rows)

    cols = [slice(k * half, (k + 1) * half) for k in (0, 1)]
    every = slice(0, d)
    partner = []

    def to_partner(yy):
        ref = S.at[core, yrows(yy)]
        partner.append(net.send(ref, ref, core=other))

    flows = {}

    def y_start(b, hh):
        if ny > 1:
            ref = S.at[core, sub(y, hh)]
            flows[b] = {s: net.send(ref, ref, y=ys[s]) for s in (1, -1)}

    def y_hop(b, hh, hop):
        if hop > hops:
            return
        for s, part in both:
            got(flows[b][s], f"y{b}_{hop}")
            if hop < hops:
                c = every if hop < hops - 1 else cols[part]
                ref = S.at[core, sub(turn(y, -s * hop, ny), hh), c]
                flows[b][s] = net.send(ref, ref, y=ys[s])
        if b == 3:
            to_partner(turn(y, -hop, ny))
            if hop < hops:
                to_partner(turn(y, hop, ny))

    w_x = {0: spread(zl, all_lanes)}
    w_far, w_z = {}, {}
    zs = [zl] + [turn(zl, -i, nz) for i in range(1, nz)]

    def relay_row(i):
        if i < nz:
            arrive(w_x[i], f"wx{i}")
            w_far[i] = relay(zs[i], all_lanes if i == 0 else gu_lanes)

    def spread_row(i):
        if i < nz:
            got(w_z[i], f"wz{i}")
            w_x[i] = spread(zs[i], gu_lanes)

    got(a_in, "a")
    S[core, sub(y, zh), :] = A[core] + AR[...]
    if nh > 1:
        ref = S.at[core, sub(y, zh)]
        z_in = {s: net.send(ref, ref, zh=hs[s]) for s in (1, -1)}
    if nz > 1:
        w_z[1] = own_to_zl(1)
    b_hh = [zh, hs[-1], hs[1], turn(zh, 2, nh)]
    near = (1, 2) if nh > 1 else ()

    def y_near(hop):
        for b in near:
            y_hop(b, b_hh[b], hop)

    y_start(0, zh)
    y_hop(0, zh, 1)
    relay_row(0)
    if nh > 1:
        arrive(z_in, "zh")
        z_far = []
        for s, part in both:
            ref = S.at[core, sub(y, hs[-s]), cols[part]]
            z_far.append(net.send(ref, ref, zh=hs[s]))
    if nz > 2:
        w_z[2] = own_to_zl(2)
    for b in near:
        y_start(b, b_hh[b])
    if nx > 1:
        for s in (1, -1):
            down_to_zl(piece(xs[s], zl))
    y_hop(0, zh, 2)
    y_near(1)
    y_hop(0, zh, 3)
    spread_row(1)
    if nh > 1:
        for copy in z_far:
            got(copy, "zfar")
        y_start(3, b_hh[3])
        to_partner(y)
    if nx > 1:
        arrive(w_far[0], "wf0")
        down_to_zl(piece(turn(x, 2, nx), zl))
    y_near(2)
    y_hop(0, zh, 4)
    if nh > 1:
        y_hop(3, b_hh[3], 1)
    relay_row(1)
    spread_row(2)
    y_near(3)
    if nh > 1:
        y_hop(3, b_hh[3], 2)
    y_near(4)
    relay_row(2)
    if nh > 1:
        y_hop(3, b_hh[3], 3)
        y_hop(3, b_hh[3], 4)
    else:
        for hop in range(1, hops + 1):
            to_partner(turn(y, -hop, ny))
            if hop < hops:
                to_partner(turn(y, hop, ny))
        to_partner(y)

    for i in range(1, nz):
        arrive(w_far[i], "wfar")
    for copy in down_in:
        got(copy, "down")
    for copy in partner:
        got(copy, "partner")

    def pack(blocks):
        shape = (2 * CAP * blocks, PAD * blocks)
        i, j = (lax.broadcasted_iota(jnp.int32, shape, k) for k in (0, 1))
        return jnp.where(j == (i // (2 * CAP)) * PAD + lax.rem(i, 2 * CAP), 1.0, 0.0).astype(BF16)

    gate_up = dot(S[0, 0:total, :], W[:, gu_lanes])
    back = dot(S[1, 0:total, :], W[:, down_lanes])
    gate, up = gate_up[:, 0:TILE], gate_up[:, TILE : 2 * TILE]
    sig = jax.nn.sigmoid(gate)
    act = gate * sig
    gate_grad = back * up * sig * (1.0 + gate * (1.0 - sig))
    up_grad = back * act
    GU[:, 0:TILE] = gate_grad.astype(BF16)
    GU[:, TILE : 2 * TILE] = up_grad.astype(BF16)
    GP[...] = dot(pack(ny * nh), GU[...]).astype(BF16)
    GT[0:TILE, :] = gate_grad.T.astype(BF16)
    GT[TILE : 2 * TILE, :] = up_grad.T.astype(BF16)
    HT[...] = (act * up).T.astype(BF16)

    step = block if half % block == 0 else TILE

    def back_part(which, put):
        for j in range(half // step):
            at = pl.multiple_of(which * half + j * step, step)
            put(j * step, dot(GP[...], W[pl.ds(at, step), gu_lanes], ((1,), (1,))))

    def put_sent(at, value):
        CX[:, at : at + step] = value.astype(BF16)

    def put_own(at, value):
        OWN[:, at : at + step] = value

    def gu_grad(xx, zz):
        return dot(GT[...], S[0, 0:total, piece(xx, zz)])

    def down_grad(xx, zz):
        return dot(HT[...], S[1, 0:total, piece(xx, zz)])

    order = [turn(zl, i, nz) for i in range(1, nz)] + [zl]
    g2_in, g1_in, gz_in, dz_in = {}, {}, [], []

    def send_far(i):
        if nx == 1 or i >= nz:
            return
        G2[i] = gu_grad(turn(x, 2, nx), order[i]).astype(BF16)
        g2_in[i] = {
            s: net.send(G2.at[i, part * TILE : (part + 1) * TILE], R2.at[part, i], x=xs[s])
            for s, part in both
        }

    def send_near(i):
        if nx == 1 or i >= nz:
            return
        arrive(g2_in[i], f"g2_{i}")
        copies = {}
        for s, part in both:
            G = gu_grad(xs[s], order[i])
            lo, hi = part * TILE, (part + 1) * TILE
            G1[part, i, lo:hi, :] = (G[lo:hi] + R2[part, i].astype(F32)).astype(BF16)
            lo, hi = (1 - part) * TILE, (2 - part) * TILE
            G1[part, i, lo:hi, :] = G[lo:hi].astype(BF16)
            copies[s] = net.send(G1.at[part, i], R1.at[part, i], x=xs[s])
        g1_in[i] = copies

    def summed_here(i):
        G = gu_grad(x, order[i])
        if nx > 1:
            arrive(g1_in[i], f"g1_{i}")
            G = G + R1[0, i].astype(F32) + R1[1, i].astype(F32)
        return G

    def to_zl(i):
        if i < nz - 1:
            GS[i] = summed_here(i).astype(BF16)
            gz_in.append(net.send(GS.at[i], GR.at[i], zl=order[i]))

    def down_zl(i):
        if i < nz - 1:
            for xx in range(nx):
                DS[i, xx] = down_grad(xx, order[i]).astype(BF16)
            dz_in.append(net.send(DS.at[i], DR.at[i], zl=order[i]))

    few = 2 * CAP * nh

    def fewrows(yy):
        return pl.ds(pl.multiple_of(yy * few, few), few)

    quarter = half // 2
    quarters = [slice(q * quarter, (q + 1) * quarter) for q in (0, 1)]
    y_in = {}

    def y_step(t):
        for kind in (0, 1):
            for s, part in both:
                far = hops + 1 - t - kind
                if far < 1:
                    continue
                q = quarters[part if kind == 0 else 1 - part]
                value = OWN[fewrows(turn(y, s * far, ny)), q]
                if t > 1:
                    got(y_in[kind, s], f"r{t}")
                    value = value + YR[part, kind, t - 2].astype(F32)
                YS[part, kind, t - 1] = value.astype(BF16)
                y_in[kind, s] = net.send(
                    YS.at[part, kind, t - 1], YR.at[part, kind, t - 1], y=ys[s]
                )

    back_part(other, put_sent)
    c_in = net.send(CX, CR, core=other)
    send_far(0)
    down_zl(0)
    send_far(1)
    back_part(core, put_own)
    got(c_in, "c")
    OWN[...] += CR[...].astype(F32)
    y_step(1)
    down_zl(1)
    send_far(2)
    send_near(0)
    for xx in range(nx):
        DG[xx] = down_grad(xx, zl)
    y_step(2)
    send_near(1)
    y_step(3)
    to_zl(0)
    y_step(4)
    send_near(2)

    mine_y = [OWN[fewrows(y), q] for q in quarters]
    for kind in (0, 1):
        for s, part in both:
            if hops > kind:
                got(y_in[kind, s], "rlast")
                q = part if kind == 0 else 1 - part
                mine_y[q] = mine_y[q] + YR[part, kind, hops - 1 - kind].astype(F32)
    for q in (0, 1):
        spread_rows = dot(pack(nh), mine_y[q].astype(BF16), ((0,), (0,)))
        ZS[:, :, quarters[q]] = spread_rows.reshape(nh, PAD, quarter).astype(BF16)

    if nh > 1:
        pl.semaphore_wait(known, 2)
        z_in = []
        for i, s in enumerate((2, 1, -1)):
            there = turn(zh, s, nh)
            z_in.append(net.send(ZS.at[there], ZR.at[i], zh=there))
    to_zl(1)

    for i, copy in enumerate(dz_in):
        got(copy, f"dz{i}")
        DG[...] += DR[i].astype(F32)
    mid = TILE // 2
    if nx > 1:
        D2[...] = DG[turn(x, 2, nx)].astype(BF16)
        d_in = {
            s: net.send(D2.at[part * mid : (part + 1) * mid], E2.at[part], x=xs[s])
            for s, part in both
        }

    if nx > 1:
        arrive(d_in, "d2")
        for s, part in both:
            lo, hi = part * mid, (part + 1) * mid
            D1[part, lo:hi, :] = (DG[xs[s], lo:hi, :] + E2[part].astype(F32)).astype(BF16)
            lo, hi = (1 - part) * mid, (2 - part) * mid
            D1[part, lo:hi, :] = DG[xs[s], lo:hi, :].astype(BF16)
            d_in[s] = net.send(D1.at[part], E1.at[part], x=xs[s])

    final = ZS[zh].astype(F32)
    if nh > 1:
        for i in (1, 2, 0):
            got(z_in[i], f"rz{i}")
        for i in range(3):
            final = final + ZR[i].astype(F32)
    FR[core] = final.astype(BF16)
    f_in = net.send(FR.at[core], FR.at[core], core=other)

    GO[...] = summed_here(nz - 1)
    for i, copy in enumerate(gz_in):
        got(copy, f"gz{i}")
        GO[...] += GR[i].astype(F32)
    for k in range(2):
        wg_ref[k] = GO[k * TILE : (k + 1) * TILE, :].T

    total_down = DG[x]
    if nx > 1:
        arrive(d_in, "d1")
        total_down = total_down + E1[0].astype(F32) + E1[1].astype(F32)
    wg_ref[2] = total_down.T

    got(f_in, "f")
    hit_b = HIT[...].astype(BF16)
    for c in (0, 1):
        ig_ref[:, cols[c]] = dot(hit_b, FR[c], ((0,), (0,))).astype(BF16)

    for copy in net.copies:
        copy.wait_send()


def per_device(sizes, out_grad, layer_input, expert_ids, gate_prob, w_stack, scale_exps):
    nx, nz, ny, nh, _ = sizes
    tokens, d = layer_input.shape
    block = w_stack.shape[1]
    half, rows, wide = d // 2, PAD * nh, 2 * TILE
    total = rows * ny
    hops, few = max(ny // 2, 1), 2 * CAP * nh
    arrays = (
        out_grad,
        layer_input,
        expert_ids.T,
        gate_prob.T,
        w_stack,
        jnp.transpose(scale_exps, (1, 2, 0)),
    )
    outs = (jax.ShapeDtypeStruct((tokens, d), BF16), jax.ShapeDtypeStruct(w_stack.shape, F32))
    scratch = [pltpu.VMEM(a.shape, a.dtype) for a in arrays] + [
        pltpu.VMEM((d, 3 * TILE), BF16),
        pltpu.VMEM((2, PAD, d), BF16),
        pltpu.VMEM((PAD, d), BF16),
        pltpu.VMEM((PAD, tokens), F32),
        pltpu.VMEM((2, total + PAD, d), BF16),
        pltpu.VMEM((total, wide), BF16),
        pltpu.VMEM((few * ny, wide), BF16),
        pltpu.VMEM((wide, total), BF16),
        pltpu.VMEM((TILE, total), BF16),
        pltpu.VMEM((few * ny, half), BF16),
        pltpu.VMEM((few * ny, half), BF16),
        pltpu.VMEM((few * ny, half), F32),
        pltpu.VMEM((2, 2, hops, few, half // 2), BF16),
        pltpu.VMEM((2, 2, hops, few, half // 2), BF16),
        pltpu.VMEM((nh, PAD, half), BF16),
        pltpu.VMEM((3, PAD, half), BF16),
        pltpu.VMEM((2, PAD, half), BF16),
        pltpu.VMEM((nz, wide, block), BF16),
        pltpu.VMEM((2, nz, TILE, block), BF16),
        pltpu.VMEM((2, nz, wide, block), BF16),
        pltpu.VMEM((2, nz, wide, block), BF16),
        pltpu.VMEM((wide, block), F32),
        pltpu.VMEM((nz, wide, block), BF16),
        pltpu.VMEM((nz, wide, block), BF16),
        pltpu.VMEM((nz, nx, TILE, block), BF16),
        pltpu.VMEM((nz, nx, TILE, block), BF16),
        pltpu.VMEM((nx, TILE, block), F32),
        pltpu.VMEM((TILE, block), BF16),
        pltpu.VMEM((2, TILE // 2, block), BF16),
        pltpu.VMEM((2, TILE, block), BF16),
        pltpu.VMEM((2, TILE, block), BF16),
        pltpu.SemaphoreType.DMA((128,)),
        pltpu.SemaphoreType.DMA((128,)),
        pltpu.SemaphoreType.DMA((6,)),
        pltpu.SemaphoreType.REGULAR,
    ]
    hbm = pl.BlockSpec(memory_space=pltpu.HBM)
    return pl.pallas_call(
        functools.partial(kernel, sizes),
        out_shape=outs,
        in_specs=[hbm] * 6,
        out_specs=(pl.BlockSpec(memory_space=pltpu.VMEM),) * 2,
        scratch_shapes=scratch,
        compiler_params=pltpu.CompilerParams(
            collective_id=0, has_side_effects=True, vmem_limit_bytes=67043328
        ),
        name="expert_backward",
    )(*arrays)


def build(devices, sizes):
    split = Mesh(devices.reshape(sizes), AXES)
    tokens = P(AXES, None)
    weights = P(None, ("x", "zl"), ("y", "zh", "core"))
    return jax.shard_map(
        functools.partial(per_device, sizes),
        mesh=split,
        in_specs=(tokens, tokens, tokens, tokens, weights, weights),
        out_specs=(tokens, weights),
        check_vma=False,
    )


def solution(mesh):
    return build(mesh.devices, SIZES)
```

time: 83.5 us -> 80.4 us (0.963)
  the two profiles are of different devices: /device:TPU:1 before, /device:TPU:137 now
where the time goes in v3:
time: 80.4 us; the launch traced here: 80.1 us
  Pallas kernels  76.2 us (95%)
  local copies, waits for them, and re-layouts  3.31 us (4%)
    pallas_call x1, Pallas kernels, per_device(): pl.pallas_call(functools.partial(kernel, sizes), out_shape=outs, in_specs...  76.2 us
    unnamed x2, local copies, waits for them, and re-layouts  3.31 us

profile of v3, /device:TPU:137, one launch (start us, length us, event | category | flops | bytes accessed | tf_op | source)
XLA Modules:
  0.0 80.1 jit_solution(16423572096542102537)
XLA Ops:
  0.6 76.2 %expert_backward.1 = (bf16[12,3072]{1,0:T(8,128)(2,1)}, f32[3,256,128]{2,1,0:T(8,128)}) custom-call(bf16[12,3072]{1,0:T(8,128)(2,1)} %og_hbm.1, bf16[12,3072]{1,0:T(8,128)(2,1)} %li_hbm.1, s32[2,12]{1,0:T(2,128)} %bitcast.3, f32[2,12]{1,0:T(2,128)} %bitcast.4, bf16[3,256,128]{2,1,0:T(8,128)(2,1)} %w_hbm.1, s32[2,1,3]{2,1,0:T(1,128)} %bitcast.5), custom_call_target="tpu_custom_call" | custom-call | tf_op jit(solution)/shard_map/expert_backward/pallas_call | solution.py:540
  76.8 1.5 %copy.10 = bf16[12,3072]{1,0:T(8,128)(2,1)} copy(bf16[12,3072]{1,0:T(8,128)(2,1)} %get-tuple-element.4) | data formatting | bytes 147456
  78.4 1.8 %copy.11 = f32[3,256,128]{2,1,0:T(8,128)} copy(f32[3,256,128]{2,1,0:T(8,128)} %get-tuple-element.5) | data formatting | bytes 786432
